TPU v7x, 32 devices: a whole 2x2x4 slice. The times are simulated.
32 devices in a mesh: grp: 2 (over y), row: 16 (over z, x, core).
Axes of the slice: x: 2, y: 2, z: 4, core: 2. Of those that a mesh axis runs over, the one named last changes fastest.
Arguments:
- queries: bfloat16 [4096, 4096], P(('grp', 'row')), parts along dimension 0, may hold values from -130 to 130
- answer_keys: bfloat16 [4096, 512], P(('grp', 'row')), parts along dimension 0, may hold values from -6 to 6
- answer_values: bfloat16 [4096, 512], P(('grp', 'row')), parts along dimension 0, may hold values from -6 to 6
- prompt_keys: bfloat16 [256, 512], P(('grp', 'row')), parts along dimension 0, may hold values from -4 to 4
- prompt_values: bfloat16 [256, 512], P(('grp', 'row')), parts along dimension 0, may hold values from -6 to 6
- out_grad: bfloat16 [4096, 4096], P(('grp', 'row')), parts along dimension 0, may hold values from -6 to 6
- weights: float32 [4096], P(('grp', 'row')), parts along dimension 0, may hold values from 0.25 to 4
- lengths: int32 [64], P('grp'), parts along dimension 0, may hold values from 1 to 256, as said below
Outputs:
- attn_out: bfloat16 [4096, 4096], P(('grp', 'row')), parts along dimension 0
- q_grad: bfloat16 [4096, 4096], P(('grp', 'row')), parts along dimension 0
- answer_key_grad: bfloat16 [4096, 512], P(('grp', 'row')), parts along dimension 0
- answer_value_grad: bfloat16 [4096, 512], P(('grp', 'row')), parts along dimension 0
- prompt_key_grad: float32 [256, 512], P(('grp', 'row')), parts along dimension 0
- prompt_value_grad: float32 [256, 512], P(('grp', 'row')), parts along dimension 0
There are 2 independent parts, one for each index of `grp`. A program takes and returns all parts, laid end to end along the dimension named above; each array names one. Nothing has to cross between parts.
Inputs may be any that keep to these rules, and one draw needn't show every extreme that they name: `lengths`: the answers fill the 2048 packed rows in order; the longest has exactly 256 rows.
All inputs are finite; a program needn't handle non-finite values.
Results may differ from a plain program's by a relative error of at most 0.02.
Values may be sent and summed in bfloat16 or wider, within the bound.
A program may use at most 192 MiB of HBM per device.

v0:
```python
import jax
import jax.numpy as jnp
from jax import lax
from jax.sharding import PartitionSpec as P

HEAD_DIM = 128


MASKED = -1e30


def shifted(x, axis, by):
    length = lax.axis_size(axis)
    pairs = [(i, i + by) for i in range(length) if 0 <= i + by < length]
    return lax.ppermute(x, axis, pairs)


def times_transposed(former, latter):
    return lax.dot_general(
        former, latter, (((1,), (1,)), ((), ())), preferred_element_type=jnp.float32
    )


def transposed_times(former, latter):
    return lax.dot_general(
        former, latter, (((0,), (0,)), ((), ())), preferred_element_type=jnp.float32
    )


def segment_of(positions, lengths):
    finish = jnp.cumsum(lengths, dtype=jnp.int32)
    starts = finish - lengths
    covered = (starts[None, :] <= positions[:, None]).astype(jnp.int32)
    return jnp.sum(covered, axis=1, dtype=jnp.int32) - 1


def probabilities(flat_queries, key_rows, allowed, group_size):
    key_count = key_rows.shape[0]
    height = allowed.shape[0]
    factor = key_rows.shape[1] ** (-0.5)
    scores = (times_transposed(flat_queries, key_rows) * factor).reshape(
        height, group_size, key_count
    )
    window = jnp.concatenate(
        [jnp.ones((height, key_count - allowed.shape[1]), dtype=jnp.bool_), allowed], axis=1
    )
    scores = jnp.where(window[:, None, :], scores, MASKED)
    highest = jnp.max(scores, axis=2, keepdims=True)
    powers = jnp.exp(scores - highest)
    totals = jnp.sum(powers, axis=2, keepdims=True)
    return ((powers / totals).reshape(height * group_size, key_count), highest, totals)


def per_device(
    queries, answer_keys, answer_values, prompt_keys, prompt_values, out_grad, weights, lengths
):
    height = queries.shape[0]
    head_dim = HEAD_DIM
    columns = answer_keys.shape[1]
    kv_heads = columns // head_dim
    group_size = queries.shape[1] // columns
    span_cols = group_size * head_dim
    factor = head_dim ** (-0.5)
    prompt_count = prompt_keys.shape[0] * lax.axis_size("row")
    device_place = lax.axis_index("row")
    own_pos = device_place * height + jnp.arange(height, dtype=jnp.int32)
    key_pos = (device_place - 2) * height + jnp.arange(3 * height, dtype=jnp.int32)
    own_seg = segment_of(own_pos, lengths)
    key_seg = segment_of(key_pos, lengths)
    allowed = (
        (key_pos[None, :] >= 0)
        & (key_pos[None, :] <= own_pos[:, None])
        & (key_seg[None, :] == own_seg[:, None])
    )
    earlier = (answer_keys, answer_values)
    received = []
    for repeat in range(2):
        earlier = shifted((earlier[0], earlier[1]), "row", 1)
        received.insert(0, earlier)
    window_keys = jnp.concatenate([received[0][0], received[1][0], answer_keys], axis=0)
    window_values = jnp.concatenate([received[0][1], received[1][1], answer_values], axis=0)
    cotangent = (weights[:, None] * out_grad.astype(jnp.float32)).astype(jnp.bfloat16)

    def head_slices(kv_index, gathered_keys, gathered_values):
        flat_queries = queries[:, kv_index * span_cols : (kv_index + 1) * span_cols].reshape(
            height * group_size, head_dim
        )
        flat_cot = cotangent[:, kv_index * span_cols : (kv_index + 1) * span_cols].reshape(
            height * group_size, head_dim
        )
        key_rows = jnp.concatenate(
            [
                gathered_keys[:, kv_index * head_dim : (kv_index + 1) * head_dim],
                window_keys[:, kv_index * head_dim : (kv_index + 1) * head_dim],
            ],
            axis=0,
        )
        value_rows = jnp.concatenate(
            [
                gathered_values[:, kv_index * head_dim : (kv_index + 1) * head_dim],
                window_values[:, kv_index * head_dim : (kv_index + 1) * head_dim],
            ],
            axis=0,
        )
        return (flat_queries, flat_cot, key_rows, value_rows)

    gathered_keys, gathered_values = (
        lax.all_gather(prompt_keys, "row", axis=0, tiled=True),
        lax.all_gather(prompt_values, "row", axis=0, tiled=True),
    )
    attended_list = []
    records = []
    for kv_index in range(kv_heads):
        flat_queries, flat_cot, key_rows, value_rows = head_slices(
            kv_index, gathered_keys, gathered_values
        )
        chances, highest, totals = probabilities(flat_queries, key_rows, allowed, group_size)
        attended_list.append(
            jnp.dot(
                chances.astype(jnp.bfloat16), value_rows, preferred_element_type=jnp.float32
            ).astype(jnp.bfloat16)
        )
    source_keys, source_values = (
        lax.all_gather(prompt_keys, "row", axis=0, tiled=True),
        lax.all_gather(prompt_values, "row", axis=0, tiled=True),
    )
    for kv_index in range(kv_heads):
        flat_queries, flat_cot, key_rows, value_rows = head_slices(
            kv_index, source_keys, source_values
        )
        chances, highest, totals = probabilities(flat_queries, key_rows, allowed, group_size)
        rounded = chances.astype(jnp.bfloat16)
        row_delta = jnp.sum(
            flat_cot.astype(jnp.float32) * attended_list[kv_index].astype(jnp.float32),
            axis=1,
            keepdims=True,
        )
        head_slopes = times_transposed(flat_cot, value_rows)
        head_score_grad = (chances * (head_slopes - row_delta)).astype(jnp.bfloat16)
        q_part = (
            jnp.dot(head_score_grad, key_rows, preferred_element_type=jnp.float32) * factor
        ).astype(jnp.bfloat16)
        key_part = transposed_times(head_score_grad[:, prompt_count:], flat_queries) * factor
        value_part = transposed_times(rounded[:, prompt_count:], flat_cot)
        q_part, key_part, value_part, row_delta = (q_part, key_part, value_part, row_delta)
        records.append((q_part, key_part, value_part, row_delta, highest, totals))
    attn_out = jnp.concatenate([item.reshape(height, span_cols) for item in attended_list], axis=1)
    q_grad = jnp.concatenate([record[0].reshape(height, span_cols) for record in records], axis=1)
    key_terms = jnp.concatenate([record[1] for record in records], axis=1)
    value_terms = jnp.concatenate([record[2] for record in records], axis=1)
    row_count = lax.axis_size("row") * prompt_keys.shape[0]
    key_parts = []
    value_parts = []
    for kv_index in range(kv_heads):
        flat_queries = queries[:, kv_index * span_cols : (kv_index + 1) * span_cols].reshape(
            height * group_size, head_dim
        )
        flat_cot = cotangent[:, kv_index * span_cols : (kv_index + 1) * span_cols].reshape(
            height * group_size, head_dim
        )
        key_piece = source_keys[:, kv_index * head_dim : (kv_index + 1) * head_dim]
        value_piece = source_values[:, kv_index * head_dim : (kv_index + 1) * head_dim]
        row_delta, highest, totals = (
            records[kv_index][3],
            records[kv_index][4],
            records[kv_index][5],
        )
        scores = (times_transposed(flat_queries, key_piece) * factor).reshape(
            height, group_size, row_count
        )
        chances = (jnp.exp(scores - highest) / totals).reshape(height * group_size, row_count)
        slopes = times_transposed(flat_cot, value_piece)
        score_grad = (chances * (slopes - row_delta)).astype(jnp.bfloat16)
        key_parts.append(transposed_times(score_grad, flat_queries) * factor)
        value_parts.append(transposed_times(chances.astype(jnp.bfloat16), flat_cot))
    stacked = lax.psum_scatter(
        jnp.concatenate(key_parts + value_parts, axis=1), "row", scatter_dimension=0, tiled=True
    )
    prompt_key_grad = stacked[:, :columns]
    prompt_value_grad = stacked[:, columns:]
    pending = (key_terms[:height], value_terms[:height])
    for nearer in (
        (key_terms[height : 2 * height], value_terms[height : 2 * height]),
        (key_terms[2 * height :], value_terms[2 * height :]),
    ):
        arrived = shifted((pending[0], pending[1]), "row", -1)
        pending = (nearer[0] + arrived[0], nearer[1] + arrived[1])
    answer_key_grad = pending[0].astype(jnp.bfloat16)
    answer_value_grad = pending[1].astype(jnp.bfloat16)
    return (
        attn_out,
        q_grad,
        answer_key_grad,
        answer_value_grad,
        prompt_key_grad,
        prompt_value_grad,
    )


def solution(mesh):
    in_specs = (
        P(("grp", "row"), None),
        P(("grp", "row"), None),
        P(("grp", "row"), None),
        P(("grp", "row"), None),
        P(("grp", "row"), None),
        P(("grp", "row"), None),
        P(("grp", "row")),
        P("grp"),
    )
    out_specs = (
        P(("grp", "row"), None),
        P(("grp", "row"), None),
        P(("grp", "row"), None),
        P(("grp", "row"), None),
        P(("grp", "row"), None),
        P(("grp", "row"), None),
    )
    return jax.shard_map(
        per_device, mesh=mesh, in_specs=in_specs, out_specs=out_specs, check_vma=False
    )
```

profile of v0, /device:TPU:0, one launch (start us, length us, event | category | flops | bytes accessed | tf_op | source)
XLA Modules:
  0.0 189.7 jit_solution(16702698366994527907)
XLA Ops:
  7.2 2.4 %collective-permute-start = (bf16[128,512]{1,0:T(8,128)(2,1)}, bf16[128,512]{1,0:T(8,128)(2,1)S(1)}, u32[]{:S(2)}, u32[]{:S(2)}) collective-permute-start(bf16[128,512]{1,0:T(8,128)(2,1)} %param.9), channel_id=1, source_target_pairs={{0,1},{1,2},{2,3},{3,4},{4,5},{5,6},{6,7},{7,8},{8,9},{9,10},{10,1... | collective-permute-start | bytes 393224 | tf_op jit(solution)/shard_map/ppermute | solution.py:15
  9.6 4.5 %collective-permute-start.2 = (bf16[128,512]{1,0:T(8,128)(2,1)}, bf16[128,512]{1,0:T(8,128)(2,1)S(1)}, u32[]{:S(2)}, u32[]{:S(2)}) collective-permute-start(bf16[128,512]{1,0:T(8,128)(2,1)} %param.10), channel_id=1, source_target_pairs={{0,1},{1,2},{2,3},{3,4},{4,5},{5,6},{6,7},{7,8},{8,9},{9,10},{10,1... | collective-permute-start | bytes 393224 | tf_op jit(solution)/shard_map/ppermute | solution.py:15
  15.9 20.6 %all_gather.9 = bf16[128,512]{1,0:T(8,128)(2,1)S(1)} all-gather(bf16[8,512]{1,0:T(8,128)(2,1)} %param.12), channel_id=1, replica_groups=mesh['grp'=2,'row'=16] {'row'}, dimensions={0}, use_global_device_ids=true | all-gather | bytes 139264 | tf_op jit(solution)/shard_map/all_gather | solution.py:109
  37.0 1.6 multiply_convert_fusion.4
  44.5 17.8 %all_gather.8 = bf16[128,512]{1,0:T(8,128)(2,1)S(1)} all-gather(bf16[8,512]{1,0:T(8,128)(2,1)S(1)} %copy-done.23), channel_id=1, replica_groups=mesh['grp'=2,'row'=16] {'row'}, dimensions={0}, use_global_device_ids=true | all-gather | bytes 139264 | tf_op jit(solution)/shard_map/all_gather | solution.py:108
  62.3 2.2 %collective-permute-start.1 = (bf16[128,512]{1,0:T(8,128)(2,1)S(1)}, bf16[128,512]{1,0:T(8,128)(2,1)S(1)}, u32[]{:S(2)}, u32[]{:S(2)}) collective-permute-start(bf16[128,512]{1,0:T(8,128)(2,1)S(1)} %collective-permute-done), channel_id=1, source_target_pairs={{0,1},{1,2},{2,3},{3,4},{4,5},{5,6},{6,7},{7,8},{8,9},{9,10},{10,1... | collective-permute-start | bytes 393224 | tf_op jit(solution)/shard_map/ppermute | solution.py:15
  64.6 3.5 %collective-permute-start.3 = (bf16[128,512]{1,0:T(8,128)(2,1)S(1)}, bf16[128,512]{1,0:T(8,128)(2,1)S(1)}, u32[]{:S(2)}, u32[]{:S(2)}) collective-permute-start(bf16[128,512]{1,0:T(8,128)(2,1)S(1)} %collective-permute-done.2), channel_id=1, source_target_pairs={{0,1},{1,2},{2,3},{3,4},{4,5},{5,6},{6,7},{7,8},{8,9},{9,10},{10,1... | collective-permute-start | bytes 393224 | tf_op jit(solution)/shard_map/ppermute | solution.py:15
  70.9 1.1 multiply_reduce_fusion.1
  72.5 1.2 fusion.30
  73.7 1.1 convolution_multiply_fusion.9
  75.7 1.2 fusion.22
  77.2 1.1 fusion.44
  78.2 1.1 multiply_reduce_fusion
  79.9 1.2 fusion.31
  81.1 1.1 convolution_multiply_fusion.8
  83.0 1.2 fusion.14
  84.5 1.1 fusion.48
  85.6 1.1 multiply_reduce_fusion.2
  87.3 1.2 fusion.29
  88.5 1.0 convolution_multiply_fusion.10
  90.4 1.2 fusion.10
  91.9 1.1 fusion.50
  93.0 1.3 multiply_reduce_fusion.3
  94.8 1.2 fusion.28
  96.0 1.0 convolution_multiply_fusion.11
  97.1 2.1 %fusion.43 = f32[128,1024]{0,1:T(8,128)} fusion(bf16[1024,128]{1,0:T(8,128)(2,1)S(1)} %reshape.229, f32[1024,128]{1,0:T(8,128)} %fusion.10, bf16[1024,128]{1,0:T(8,128)(2,1)S(1)} %reshape.237, f32[1024]{0:T(1024)S(1)} %get-tuple-element.70, bf16[128,512]{1,0:T(8,128)(2,1)S(1)} %all_gather.9), kind=kOutput, calls=%fused_computation.80 | convolution fusion | flops 67518464 | bytes 1150976 | tf_op jit(solution)/shard_map/dot_general | solution.py:25
  99.2 2.1 %fusion.41 = f32[128,1024]{0,1:T(8,128)} fusion(f32[128,1024]{0,1:T(8,128)} %fusion.43, bf16[1024,128]{1,0:T(8,128)(2,1)S(1)} %reshape.231, f32[1024,128]{1,0:T(8,128)} %fusion.14, bf16[1024,128]{1,0:T(8,128)(2,1)S(1)} %reshape.239, f32[1024]{0:T(1024)S(1)} %get-tuple-element.68, bf16[128,512]{1,0:T(8,128)(2,1)S(1)} %all_gather.9), kind=kOutput, calls=%fused_computation.78 | convolution fusion | flops 67518464 | bytes 1150976 | tf_op jit(solution)/shard_map/dot_general | solution.py:25
  101.3 1.1 fusion.39
  102.4 1.1 fusion.37
  103.5 2.0 %convolution_dynamic-update-slice_fusion.3 = f32[128,1024]{0,1:T(8,128)} fusion(f32[128,1024]{0,1:T(8,128)} %fusion.37, bf16[1024,128]{1,0:T(8,128)(2,1)S(1)} %reshape.237, f32[1024,128]{1,0:T(8,128)} %fusion.10), kind=kOutput, calls=%fused_computation.72 | convolution fusion | flops 33685504 | bytes 851968 | tf_op jit(solution)/shard_map/dot_general | solution.py:25
  108.2 1.4 collective-permute-start.6
  110.4 1.3 collective-permute-start.4
  113.4 1.1 reshape.244
  114.4 1.1 copy.69
  115.7 1.1 reshape.240
  116.8 1.8 copy.67
  118.5 1.1 reshape.230
  119.6 1.8 reshape.238
  121.4 2.0 %copy.90 = f32[128,1024]{1,0:T(8,128)} copy(f32[128,1024]{0,1:T(8,128)} %convolution_dynamic-update-slice_fusion) | data formatting | bytes 1048576
  123.5 1.0 slice_add_fusion
  124.4 1.3 collective-permute-start.7
  125.8 1.7 slice_add_fusion.2
  127.4 1.3 collective-permute-start.5
  128.7 2.4 %pad_maximum_fusion = (bf16[128,4096]{1,0:T(8,128)(2,1)}, bf16[128,4096]{1,0:T(8,128)(2,1)}) fusion(bf16[128,1024]{1,0:T(8,128)(2,1)S(1)} %reshape.236, bf16[128,1024]{1,0:T(8,128)(2,1)S(1)} %reshape.234, bf16[128,1024]{1,0:T(8,128)(2,1)S(1)} %reshape.232, bf16[128,1024]{1,0:T(8,128)(2,1)S(1)} %reshape.230, bf16[128,1024]{1,0:T(8,128)(2,1)S(1)} %reshape.244, ...), kind=kLoop, calls=%fused_computation.81 | loop fusion | flops 8388608 | bytes 4194304 | tf_op jit(solution)/shard_map/concatenate | solution.py:147
  132.0 1.1 collective-permute-done.5
  133.1 1.0 fusion.61
  134.8 46.7 %reduce-scatter.4.cloned.1.call-done = f32[8,1024]{1,0:T(8,128)} async-done(((f32[128,1024]{1,0:T(8,128)}), f32[8,1024]{1,0:T(8,128)}) %reduce-scatter.4.cloned.1.call-update) | async-done | bytes 32784
  181.5 1.3 fusion.104
  (130 shorter events, 23.2 us)
Async XLA Ops:
  7.2 174.4 %reduce-scatter.4.cloned.1.call-start = ((), (), s32[]{:S(2)}) async-start(), calls=%async_computation.1 | async-start | bytes 557056
  7.2 55.1 %collective-permute-start = (bf16[128,512]{1,0:T(8,128)(2,1)}, bf16[128,512]{1,0:T(8,128)(2,1)S(1)}, u32[]{:S(2)}, u32[]{:S(2)}) collective-permute-start(bf16[128,512]{1,0:T(8,128)(2,1)} %param.9), channel_id=1, source_target_pairs={{0,1},{1,2},{2,3},{3,4},{4,5},{5,6},{6,7},{7,8},{8,9},{9,10},{10,1... | collective-permute-start | bytes 393224 | tf_op jit(solution)/shard_map/ppermute | solution.py:15
  9.6 54.9 %collective-permute-start.2 = (bf16[128,512]{1,0:T(8,128)(2,1)}, bf16[128,512]{1,0:T(8,128)(2,1)S(1)}, u32[]{:S(2)}, u32[]{:S(2)}) collective-permute-start(bf16[128,512]{1,0:T(8,128)(2,1)} %param.10), channel_id=1, source_target_pairs={{0,1},{1,2},{2,3},{3,4},{4,5},{5,6},{6,7},{7,8},{8,9},{9,10},{10,1... | collective-permute-start | bytes 393224 | tf_op jit(solution)/shard_map/ppermute | solution.py:15
  37.0 1.7 copy-start.2
  40.5 3.9 %copy-start.23 = (bf16[8,512]{1,0:T(8,128)(2,1)S(1)}, bf16[8,512]{1,0:T(8,128)(2,1)}, u32[]{:S(2)}) copy-start(bf16[8,512]{1,0:T(8,128)(2,1)} %param.11) | copy-start | bytes 24580
  42.3 25.9 %copy-start.17 = (bf16[128,512]{1,0:T(8,128)(2,1)S(1)}, bf16[128,512]{1,0:T(8,128)(2,1)}, u32[]{:S(2)}) copy-start(bf16[128,512]{1,0:T(8,128)(2,1)} %param.9) | copy-start | bytes 393220
  62.3 5.8 %collective-permute-start.1 = (bf16[128,512]{1,0:T(8,128)(2,1)S(1)}, bf16[128,512]{1,0:T(8,128)(2,1)S(1)}, u32[]{:S(2)}, u32[]{:S(2)}) collective-permute-start(bf16[128,512]{1,0:T(8,128)(2,1)S(1)} %collective-permute-done), channel_id=1, source_target_pairs={{0,1},{1,2},{2,3},{3,4},{4,5},{5,6},{6,7},{7,8},{8,9},{9,10},{10,1... | collective-permute-start | bytes 393224 | tf_op jit(solution)/shard_map/ppermute | solution.py:15
  64.6 5.3 %collective-permute-start.3 = (bf16[128,512]{1,0:T(8,128)(2,1)S(1)}, bf16[128,512]{1,0:T(8,128)(2,1)S(1)}, u32[]{:S(2)}, u32[]{:S(2)}) collective-permute-start(bf16[128,512]{1,0:T(8,128)(2,1)S(1)} %collective-permute-done.2), channel_id=1, source_target_pairs={{0,1},{1,2},{2,3},{3,4},{4,5},{5,6},{6,7},{7,8},{8,9},{9,10},{10,1... | collective-permute-start | bytes 393224 | tf_op jit(solution)/shard_map/ppermute | solution.py:15
  69.5 0.9 copy-start.18
  69.5 1.4 copy-start.16
  69.5 1.4 copy-start.22
  76.8 1.4 copy-start.15
  76.8 1.4 copy-start.21
  84.2 1.4 copy-start.14
  84.2 1.4 copy-start.20
  91.5 1.4 copy-start.10
  91.5 1.4 copy-start.19
  96.0 6.4 %copy-start = (f32[1024,128]{1,0:T(8,128)S(1)}, f32[1024,128]{1,0:T(8,128)}, u32[]{:S(2)}) copy-start(f32[1024,128]{1,0:T(8,128)} %fusion.22) | copy-start | bytes 1572868
  101.3 4.2 %copy-start.1 = (f32[1024,128]{1,0:T(8,128)S(1)}, f32[1024,128]{1,0:T(8,128)}, u32[]{:S(2)}) copy-start(f32[1024,128]{1,0:T(8,128)} %fusion.14) | copy-start | bytes 1572868
  103.5 3.9 %copy-start.4 = (f32[384,128]{0,1:T(8,128)S(1)}, f32[384,128]{0,1:T(8,128)}, u32[]{:S(2)}) copy-start(f32[384,128]{0,1:T(8,128)} %fusion.44) | copy-start | bytes 589828
  103.5 3.9 %copy-start.6 = (f32[384,128]{0,1:T(8,128)S(1)}, f32[384,128]{0,1:T(8,128)}, u32[]{:S(2)}) copy-start(f32[384,128]{0,1:T(8,128)} %fusion.48) | copy-start | bytes 589828
  103.5 3.9 %copy-start.8 = (f32[384,128]{0,1:T(8,128)S(1)}, f32[384,128]{0,1:T(8,128)}, u32[]{:S(2)}) copy-start(f32[384,128]{0,1:T(8,128)} %fusion.50) | copy-start | bytes 589828
  105.5 4.1 %copy-start.3 = (f32[384,128]{0,1:T(8,128)S(1)}, f32[384,128]{0,1:T(8,128)}, u32[]{:S(2)}) copy-start(f32[384,128]{0,1:T(8,128)} %convolution_multiply_fusion.9) | copy-start | bytes 589828
  105.6 4.1 %copy-start.5 = (f32[384,128]{0,1:T(8,128)S(1)}, f32[384,128]{0,1:T(8,128)}, u32[]{:S(2)}) copy-start(f32[384,128]{0,1:T(8,128)} %convolution_multiply_fusion.8) | copy-start | bytes 589828
  105.6 4.1 %copy-start.7 = (f32[384,128]{0,1:T(8,128)S(1)}, f32[384,128]{0,1:T(8,128)}, u32[]{:S(2)}) copy-start(f32[384,128]{0,1:T(8,128)} %convolution_multiply_fusion.10) | copy-start | bytes 589828
  105.6 4.1 %copy-start.9 = (f32[384,128]{0,1:T(8,128)S(1)}, f32[384,128]{0,1:T(8,128)}, u32[]{:S(2)}) copy-start(f32[384,128]{0,1:T(8,128)} %convolution_multiply_fusion.11) | copy-start | bytes 589828
  107.5 5.2 %copy-start.11 = (bf16[1024,128]{0,1:T(8,128)(2,1)S(1)}, bf16[1024,128]{0,1:T(8,128)(2,1)}, u32[]{:S(2)}) copy-start(bf16[1024,128]{0,1:T(8,128)(2,1)} %get-tuple-element.67) | copy-start | bytes 786436
  108.2 4.8 %copy-start.12 = (bf16[1024,128]{1,0:T(8,128)(2,1)S(1)}, bf16[1024,128]{1,0:T(8,128)(2,1)}, u32[]{:S(2)}) copy-start(bf16[1024,128]{1,0:T(8,128)(2,1)} %fusion.30) | copy-start | bytes 786436
  108.2 4.9 %copy-start.13 = (bf16[1024,128]{0,1:T(8,128)(2,1)S(1)}, bf16[1024,128]{0,1:T(8,128)(2,1)}, u32[]{:S(2)}) copy-start(bf16[1024,128]{0,1:T(8,128)(2,1)} %get-tuple-element.65) | copy-start | bytes 786436
  108.2 15.3 %collective-permute-start.6 = (f32[128,512]{0,1:T(8,128)}, f32[128,512]{0,1:T(8,128)}, u32[]{:S(2)}, u32[]{:S(2)}) collective-permute-start(f32[128,512]{0,1:T(8,128)} %slice.229), channel_id=1, source_target_pairs={{1,0},{2,1},{3,2},{4,3},{5,4},{6,5},{7,6},{8,7},{9,8},{10,9},{11,1... | collective-permute-start | bytes 786440 | tf_op jit(solution)/shard_map/ppermute | solution.py:15
  110.4 15.3 %collective-permute-start.4 = (f32[128,512]{0,1:T(8,128)}, f32[128,512]{0,1:T(8,128)}, u32[]{:S(2)}, u32[]{:S(2)}) collective-permute-start(f32[128,512]{0,1:T(8,128)} %slice.222), channel_id=1, source_target_pairs={{1,0},{2,1},{3,2},{4,3},{5,4},{6,5},{7,6},{8,7},{9,8},{10,9},{11,1... | collective-permute-start | bytes 786440 | tf_op jit(solution)/shard_map/ppermute | solution.py:15
  124.4 6.7 %collective-permute-start.7 = (f32[128,512]{0,1:T(8,128)S(1)}, f32[128,512]{0,1:T(8,128)S(1)}, u32[]{:S(2)}, u32[]{:S(2)}) collective-permute-start(f32[128,512]{0,1:T(8,128)S(1)} %slice_add_fusion), channel_id=1, source_target_pairs={{1,0},{2,1},{3,2},{4,3},{5,4},{6,5},{7,6},{8,7},{9,8},{10,9},{11,1... | collective-permute-start | bytes 786440 | tf_op jit(solution)/shard_map/ppermute | solution.py:15
  127.4 5.7 %collective-permute-start.5 = (f32[128,512]{0,1:T(8,128)}, f32[128,512]{0,1:T(8,128)}, u32[]{:S(2)}, u32[]{:S(2)}) collective-permute-start(f32[128,512]{0,1:T(8,128)} %slice_add_fusion.2), channel_id=1, source_target_pairs={{1,0},{2,1},{3,2},{4,3},{5,4},{6,5},{7,6},{8,7},{9,8},{10,9},{11,1... | collective-permute-start | bytes 786440 | tf_op jit(solution)/shard_map/ppermute | solution.py:15
Sparse Core Ops, SparseCore 0:
  123.6 57.9 reduce-scatter.3
where the time goes:
time: 191 us; the launch traced here: 190 us
  waiting for transfers between devices  47.8 us (25%)
  blocking collectives  38.4 us (20%)
  matrix products  36.5 us (19%)
  local copies, waits for them, and re-layouts  22.6 us (12%)
  starting transfers between devices  18 us (9%)
  between operations  14.7 us (8%)
  other arithmetic  11.6 us (6%)
    unnamed x2, waiting for transfers between devices  46.7 us
    all_gather x1, blocking collectives, per_device(): lax.all_gather(prompt_values, 'row', axis=0, tiled=True)  20.6 us
    dot_general x16, matrix products, transposed_times(): lax.dot_general(former, latter, (((0,), (0,)), ((), ())), preferred_eleme...  19 us
    ppermute x8, starting transfers between devices, shifted(): return lax.ppermute(x, axis, pairs)  18 us
    all_gather x1, blocking collectives, per_device(): lax.all_gather(prompt_keys, 'row', axis=0, tiled=True)  17.8 us
    dot_general x12, matrix products, times_transposed(): lax.dot_general(former, latter, (((1,), (1,)), ((), ())), preferred_eleme...  8.16 us
    dot_general x4, matrix products, per_device(): jnp.dot(head_score_grad, key_rows, preferred_element_type=jnp.float32)  4.85 us
    dot_general x4, matrix products, per_device(): jnp.dot(chances.astype(jnp.bfloat16), value_rows, preferred_element_type=...  4.53 us
  transfers between devices with their start and end apart: 9, of which 2 were waited for; matrix products, arithmetic and copies ran while one was open for 16% of the time, Pallas kernels for 0%

commit v1 on v0

v1 whole, which is shorter than its diff:
```python
import functools
import math

import jax
import jax.numpy as jnp
from jax import lax
from jax.experimental import pallas as pl
from jax.experimental.pallas import tpu as pltpu
from jax.sharding import PartitionSpec as P

HEAD_DIM = 128
MASKED = -1e30
MESH = pl.DeviceIdType.MESH
NT = (((1,), (1,)), ((), ()))


def dot(a, b):
    return jnp.dot(a, b, preferred_element_type=jnp.float32)


def twice(x):
    return jnp.concatenate([x, x], axis=1)


def kernel(
    n, kv_heads, group,
    q_hbm, og_hbm, ak, av, pk, pv, w, lens,
    attn_hbm, dq_hbm, akg, avg, pkg, pvg,
    qv, ogv, attn_v, dq_v, win, pst, pgath, psend, precv, gsend, grecv, own,
    qs, cots, kcat, vcat, kt, vt, p_all, ds_all, bias, tri_b, wfull,
    in_sem, out_sem, st_sem, win_send, win_recv, pg_send, pg_recv,
    pr_send, pr_recv, gr_send, gr_recv,
):
    me = lax.axis_index("row")
    height = ak.shape[0]
    d = HEAD_DIM
    span = group * d
    prompt = pk.shape[0] * n
    factor = d ** (-0.5)
    log_factor = factor * math.log2(math.e)

    def peer(k):
        return lax.rem(me + k, n)

    def cols(g, width):
        return pl.ds(pl.multiple_of(g * width, width), width)

    def in_copies(g):
        return (
            pltpu.make_async_copy(q_hbm.at[:, cols(g, span)], qv.at[g], in_sem.at[g, 0]),
            pltpu.make_async_copy(og_hbm.at[:, cols(g, span)], ogv.at[g], in_sem.at[g, 1]),
        )

    def out_copies(g):
        return (
            pltpu.make_async_copy(attn_v.at[g], attn_hbm.at[:, cols(g, span)], out_sem.at[g, 0]),
            pltpu.make_async_copy(dq_v.at[g], dq_hbm.at[:, cols(g, span)], out_sem.at[g, 1]),
        )

    def stage_copies(g):
        return (
            pltpu.make_async_copy(pk.at[:, cols(g, d)], pst.at[g, 0], st_sem.at[g, 0]),
            pltpu.make_async_copy(pv.at[:, cols(g, d)], pst.at[g, 1], st_sem.at[g, 1]),
        )

    def win_copy(g, far, which):
        return pltpu.make_async_remote_copy(
            src_ref=(ak, av)[which].at[:, cols(g, d)],
            dst_ref=win.at[g, far, which],
            send_sem=win_send.at[g, far, which],
            recv_sem=win_recv.at[g, far, which],
            device_id={"row": peer(1 + far)},
            device_id_type=MESH,
        )

    def gather_copy(g, k):
        return pltpu.make_async_remote_copy(
            src_ref=pst.at[g],
            dst_ref=pgath.at[g, me],
            send_sem=pg_send.at[g],
            recv_sem=pg_recv.at[g],
            device_id={"row": peer(k)},
            device_id_type=MESH,
        )

    def reduce_copy(g, k):
        return pltpu.make_async_remote_copy(
            src_ref=psend.at[g, peer(k)],
            dst_ref=precv.at[g, me],
            send_sem=pr_send.at[g],
            recv_sem=pr_recv.at[g],
            device_id={"row": peer(k)},
            device_id_type=MESH,
        )

    def back_copy(g, far):
        return pltpu.make_async_remote_copy(
            src_ref=gsend.at[g, far],
            dst_ref=grecv.at[g, far],
            send_sem=gr_send.at[g, far],
            recv_sem=gr_recv.at[g, far],
            device_id={"row": peer(n - 1 - far)},
            device_id_type=MESH,
        )

    barrier = pltpu.get_barrier_semaphore()

    @pl.loop(1, n)
    def _(k):
        pl.semaphore_signal(barrier, inc=1, device_id={"row": peer(k)}, device_id_type=MESH)

    for g in range(kv_heads):
        for copy in stage_copies(g):
            copy.start()
    for g in range(kv_heads):
        for copy in in_copies(g):
            copy.start()

    answers = lens.shape[1]
    row = lax.broadcasted_iota(jnp.int32, (answers, answers), 0)
    col = lax.broadcasted_iota(jnp.int32, (answers, answers), 1)
    starts = jnp.sum(
        jnp.where(col < row, jnp.broadcast_to(lens[...], (answers, answers)), 0),
        axis=1, keepdims=True,
    )
    pos = me * height + lax.broadcasted_iota(jnp.int32, (1, height), 1)
    first = jnp.max(jnp.where(starts <= pos, starts, 0), axis=0, keepdims=True)
    key = lax.broadcasted_iota(jnp.int32, (height, height), 0)
    query = lax.broadcasted_iota(jnp.int32, (height, height), 1)
    tri = key <= query
    base = me * height
    near = jnp.where(key + (base - height) >= first, 0.0, MASKED)
    both = jnp.where(tri, key + base, key + (base - 2 * height))
    both = jnp.where(both >= first, 0.0, MASKED)
    bias[0] = near
    bias[1] = both
    tri_b[...] = tri.astype(jnp.float32).astype(jnp.bfloat16)
    wfull[...] = jnp.broadcast_to(w[...], (height, height)).T

    for g in range(kv_heads):
        for copy in stage_copies(g):
            copy.wait()
    pl.semaphore_wait(barrier, n - 1)

    @pl.loop(0, kv_heads)
    def _(g):
        pltpu.make_async_copy(pst.at[g], pgath.at[g, me], pg_recv.at[g]).start()

        @pl.loop(1, n)
        def _(k):
            gather_copy(g, k).start()

        for far in range(2):
            for which in range(2):
                win_copy(g, far, which).start()

    @pl.loop(0, kv_heads)
    def _(g):
        for copy in in_copies(g):
            copy.wait()
        for h in range(group):
            lanes = slice(h * d, (h + 1) * d)
            rows = slice(h * height, (h + 1) * height)
            qs[rows, :] = qv[g, :, lanes]
            cots[rows, :] = (wfull[...] * ogv[g, :, lanes].astype(jnp.float32)).astype(jnp.bfloat16)
        pltpu.make_async_copy(pgath.at[g], pgath.at[g], pg_recv.at[g]).wait()
        for far in range(2):
            for which in range(2):
                win_copy(g, far, which).wait_recv()
        at1, at2, at3 = prompt, prompt + height, prompt + 2 * height
        for which, (cat, tr, mine) in enumerate(((kcat, kt, ak), (vcat, vt, av))):
            gathered = pgath[g, :, which].astype(jnp.float32).reshape(prompt, d)
            cat[:at1, :] = gathered.astype(jnp.bfloat16)
            cat[at1:at2, :] = win[g, 0, which]
            cat[at2:at3, :] = win[g, 1, which]
            cat[at3:, :] = mine[:, cols(g, d)]
            tr[...] = cat[...].T
        tri2 = twice(tri)
        for pair in range(group // 2):
            rows = slice(pair * 2 * height, (pair + 1) * 2 * height)
            s = lax.dot_general(kcat[...], qs[rows, :], NT, preferred_element_type=jnp.float32)
            s_p = s[:at1]
            s_1 = s[at1:at2] + twice(bias[0])
            s_c = jnp.where(tri2, s[at3:], s[at2:at3]) + twice(bias[1])
            top = jnp.maximum(
                jnp.maximum(jnp.max(s_p, axis=0, keepdims=True), jnp.max(s_1, axis=0, keepdims=True)),
                jnp.max(s_c, axis=0, keepdims=True),
            )
            e_p = jnp.exp2((s_p - top) * log_factor)
            e_1 = jnp.exp2((s_1 - top) * log_factor)
            e_c = jnp.exp2((s_c - top) * log_factor)
            total = (
                jnp.sum(e_p, axis=0, keepdims=True)
                + jnp.sum(e_1, axis=0, keepdims=True)
                + jnp.sum(e_c, axis=0, keepdims=True)
            )
            inv = 1.0 / total
            c_p, c_1, c_c = e_p * inv, e_1 * inv, e_c * inv
            trib2 = twice(tri_b[...])
            p_all[:at1, rows] = c_p.astype(jnp.bfloat16)
            p_all[at1:at2, rows] = c_1.astype(jnp.bfloat16)
            b_c = c_c.astype(jnp.bfloat16)
            b_d = b_c * trib2
            p_all[at2:at3, rows] = b_c - b_d
            p_all[at3:, rows] = b_d
            out_t = dot(vt[...], p_all[:, rows]).astype(jnp.bfloat16)
            cot_t = cots[rows, :].T
            delta = jnp.sum(
                cot_t.astype(jnp.float32) * out_t.astype(jnp.float32), axis=0, keepdims=True
            )
            slopes = dot(vcat[...], cot_t)
            ds_all[:at1, rows] = (c_p * (slopes[:at1] - delta)).astype(jnp.bfloat16)
            ds_all[at1:at2, rows] = (c_1 * (slopes[at1:at2] - delta)).astype(jnp.bfloat16)
            s_c = jnp.where(tri2, slopes[at3:], slopes[at2:at3])
            g_c = (c_c * (s_c - delta)).astype(jnp.bfloat16)
            g_d = g_c * trib2
            ds_all[at2:at3, rows] = g_c - g_d
            ds_all[at3:, rows] = g_d
            dq_t = (dot(kt[...], ds_all[:, rows]) * factor).astype(jnp.bfloat16)
            out, dq = out_t.T, dq_t.T
            for j in range(2):
                lanes = slice((2 * pair + j) * d, (2 * pair + j + 1) * d)
                attn_v[g, :, lanes] = out[j * height : (j + 1) * height]
                dq_v[g, :, lanes] = dq[j * height : (j + 1) * height]
        for copy in out_copies(g):
            copy.start()
        for which in range(2):
            if which == 0:
                part = dot(ds_all[...], qs[...]) * factor
            else:
                part = dot(p_all[...], cots[...])
            psend[g, :, which] = part[:at1].reshape(n, prompt // n, d).astype(jnp.bfloat16)
            gsend[g, 0, which] = part[at1:at2].astype(jnp.bfloat16)
            gsend[g, 1, which] = part[at2:at3].astype(jnp.bfloat16)
            own[g, which] = part[at3:]
        back_copy(g, 1).start()
        back_copy(g, 0).start()
        pltpu.make_async_copy(psend.at[g, me], precv.at[g, me], pr_recv.at[g]).start()

        @pl.loop(1, n)
        def _(k):
            reduce_copy(g, k).start()

    for g in range(kv_heads):
        lanes = slice(g * d, (g + 1) * d)
        for far in range(2):
            back_copy(g, far).wait_recv()
        for which, grad in enumerate((akg, avg)):
            grad[:, lanes] = (
                own[g, which]
                + grecv[g, 0, which].astype(jnp.float32)
                + grecv[g, 1, which].astype(jnp.float32)
            ).astype(jnp.bfloat16)
        pltpu.make_async_copy(precv.at[g], precv.at[g], pr_recv.at[g]).wait()
        for which, grad in enumerate((pkg, pvg)):
            grad[:, lanes] = jnp.sum(precv[g, :, which].astype(jnp.float32), axis=0)

    for g in range(kv_heads):
        for copy in out_copies(g):
            copy.wait()
        for far in range(2):
            back_copy(g, far).wait_send()
            for which in range(2):
                win_copy(g, far, which).wait_send()
        sent = pgath.at[g, pl.ds(0, n - 1)]
        pltpu.make_async_copy(sent, sent, pg_send.at[g]).wait()
        sent = precv.at[g, pl.ds(0, n - 1)]
        pltpu.make_async_copy(sent, sent, pr_send.at[g]).wait()


def per_device(n, queries, answer_keys, answer_values, prompt_keys, prompt_values, out_grad, weights, lengths):
    height = queries.shape[0]
    d = HEAD_DIM
    columns = answer_keys.shape[1]
    kv_heads = columns // d
    group = queries.shape[1] // columns
    own_prompt = prompt_keys.shape[0]
    keys = own_prompt * n + 3 * height
    span = group * d
    bf16, f32 = jnp.bfloat16, jnp.float32
    vmem = pl.BlockSpec(memory_space=pltpu.VMEM)
    hbm = pl.BlockSpec(memory_space=pl.ANY)
    dma = pltpu.SemaphoreType.DMA
    return pl.pallas_call(
        functools.partial(kernel, n, kv_heads, group),
        out_shape=(
            jax.ShapeDtypeStruct(queries.shape, bf16),
            jax.ShapeDtypeStruct(queries.shape, bf16),
            jax.ShapeDtypeStruct(answer_keys.shape, bf16),
            jax.ShapeDtypeStruct(answer_keys.shape, bf16),
            jax.ShapeDtypeStruct(prompt_keys.shape, f32),
            jax.ShapeDtypeStruct(prompt_keys.shape, f32),
        ),
        in_specs=[hbm, hbm] + [vmem] * 6,
        out_specs=(hbm, hbm) + (vmem,) * 4,
        scratch_shapes=[
            pltpu.VMEM((kv_heads, height, span), bf16),
            pltpu.VMEM((kv_heads, height, span), bf16),
            pltpu.VMEM((kv_heads, height, span), bf16),
            pltpu.VMEM((kv_heads, height, span), bf16),
            pltpu.VMEM((kv_heads, 2, 2, height, d), bf16),
            pltpu.VMEM((kv_heads, 2, own_prompt, d), bf16),
            pltpu.VMEM((kv_heads, n, 2, own_prompt, d), bf16),
            pltpu.VMEM((kv_heads, n, 2, own_prompt, d), bf16),
            pltpu.VMEM((kv_heads, n, 2, own_prompt, d), bf16),
            pltpu.VMEM((kv_heads, 2, 2, height, d), bf16),
            pltpu.VMEM((kv_heads, 2, 2, height, d), bf16),
            pltpu.VMEM((kv_heads, 2, height, d), f32),
            pltpu.VMEM((group * height, d), bf16),
            pltpu.VMEM((group * height, d), bf16),
            pltpu.VMEM((keys, d), bf16),
            pltpu.VMEM((keys, d), bf16),
            pltpu.VMEM((d, keys), bf16),
            pltpu.VMEM((d, keys), bf16),
            pltpu.VMEM((keys, group * height), bf16),
            pltpu.VMEM((keys, group * height), bf16),
            pltpu.VMEM((2, height, height), f32),
            pltpu.VMEM((height, height), bf16),
            pltpu.VMEM((height, height), f32),
            dma((kv_heads, 2)),
            dma((kv_heads, 2)),
            dma((kv_heads, 2)),
            dma((kv_heads, 2, 2)),
            dma((kv_heads, 2, 2)),
            dma((kv_heads,)),
            dma((kv_heads,)),
            dma((kv_heads,)),
            dma((kv_heads,)),
            dma((kv_heads, 2)),
            dma((kv_heads, 2)),
        ],
        compiler_params=pltpu.CompilerParams(
            collective_id=0, has_side_effects=True, vmem_limit_bytes=60 * 1024 * 1024
        ),
    )(
        queries, out_grad, answer_keys, answer_values, prompt_keys, prompt_values,
        weights.reshape(1, height), lengths.reshape(1, lengths.shape[0]),
    )


def solution(mesh):
    both = ("grp", "row")
    wide = P(both, None)
    return jax.shard_map(
        functools.partial(per_device, mesh.shape["row"]),
        mesh=mesh,
        in_specs=(wide,) * 6 + (P(both), P("grp")),
        out_specs=(wide,) * 6,
        check_vma=False,
    )
```

time: 191 us -> 44.8 us (0.23)
  waiting for transfers between devices: 47.8 us -> 0 us
  blocking collectives: 38.4 us -> 0 us
  Pallas kernels: 0 us -> 37.4 us
  matrix products: 36.5 us -> 0 us
  starting transfers between devices: 18 us -> 0 us
  local copies, waits for them, and re-layouts: 22.6 us -> 6.4 us
  between operations: 14.7 us -> 0.66 us
  other arithmetic: 11.6 us -> 0 us
    unnamed x2 -> x0, waiting for transfers between devices: 46.7 us -> none
    all_gather x2 -> x0, blocking collectives: 38.4 us -> none  [the longest x1 20.6 us: per_device(): lax.all_gather(prompt_values, 'row', axis=0, tiled=True)]
    pallas_call x0 -> x1, Pallas kernels: none -> 37.4 us  [per_device(): pl.pallas_call(functools.partial(kernel, n, kv_heads, group), out_shape=(...]
    dot_general x36 -> x0, matrix products: 36.5 us -> none  [the longest x16 19 us: transposed_times(): lax.dot_general(former, latter, (((0,), (0,)), ((), ())), preferred_eleme...]
    ppermute x8 -> x0, starting transfers between devices: 18 us -> none  [shifted(): return lax.ppermute(x, axis, pairs)]
    reshape x20 -> x0, local copies, waits for them, and re-layouts: 9.82 us -> none  [the longest x4 4.04 us: per_device(): record[0].reshape(height, span_cols)]
    convert_element_type x7 -> x0, other arithmetic: 3.92 us -> none  [the longest x1 1.57 us: per_device(): (weights[:, None] * out_grad.astype(jnp.float32)).astype(jnp.bfloat16)]
    slice x9 -> x0, local copies, waits for them, and re-layouts: 3.76 us -> none  [the longest x2 1.44 us: per_device(): pending = (key_terms[:height], value_terms[:height])]
  transfers between devices with their start and end apart: 9 -> 0, of which waited for: 2 -> 0; matrix products, arithmetic and copies ran while one was open for 16% -> 0% of each run, Pallas kernels for 0% -> 0%
where the time goes in v1:
time: 44.8 us; the launch traced here: 44.5 us
  Pallas kernels  37.4 us (83%)
  local copies, waits for them, and re-layouts  6.4 us (14%)
  between operations  0.66 us (1%)
    pallas_call x1, Pallas kernels, per_device(): pl.pallas_call(functools.partial(kernel, n, kv_heads, group), out_shape=(...  37.4 us
    unnamed x16, local copies, waits for them, and re-layouts  6.4 us

profile of v1, /device:TPU:0, one launch (start us, length us, event | category | flops | bytes accessed | tf_op | source)
XLA Modules:
  0.0 44.5 jit_solution(15429469453639170544)
XLA Ops:
  0.6 37.4 %shard_map.127 = (bf16[128,4096]{1,0:T(8,128)(2,1)}, bf16[128,4096]{1,0:T(8,128)(2,1)}, bf16[128,512]{1,0:T(8,128)(2,1)}, bf16[128,512]{1,0:T(8,128)(2,1)}, f32[8,512]{1,0:T(8,128)}, /*index=5*/f32[8,512]{1,0:T(8,128)}) custom-call(bf16[128,4096]{1,0:T(8,128)(2,1)} %q_hbm.1, bf16[128,4096]{1,0:T(8,128)(2,1)} %og_hbm.1, bf16[128,512]{1,0:T(8,128)(2,1)} %ak.1, ...), custom_call_target="tpu_custom_call" | custom-call | tf_op jit(solution)/shard_map/pallas_call | solution.py:284
  38.1 0.0 copy-start
  38.1 2.4 %copy.20 = bf16[128,4096]{1,0:T(8,128)(2,1)} copy(bf16[128,4096]{1,0:T(8,128)(2,1)} %get-tuple-element.12) | data formatting | bytes 2097152
  40.4 0.0 copy-done
  40.4 0.0 copy-start.2
  40.4 1.0 %copy.21 = bf16[128,4096]{1,0:T(8,128)(2,1)} copy(bf16[128,4096]{1,0:T(8,128)(2,1)S(1)} %copy-done) | data formatting | bytes 2097152
  41.4 0.1 copy-done.2
  41.5 0.0 copy-start.1
  41.5 0.7 %copy.22 = bf16[128,512]{1,0:T(8,128)(2,1)} copy(bf16[128,512]{1,0:T(8,128)(2,1)S(1)} %copy-done.2) | data formatting | bytes 262144
  42.1 0.3 copy-done.1
  42.4 0.0 copy-start.4
  42.4 0.7 %copy.23 = bf16[128,512]{1,0:T(8,128)(2,1)} copy(bf16[128,512]{1,0:T(8,128)(2,1)S(1)} %copy-done.1) | data formatting | bytes 262144
  43.1 0.1 copy-done.4
  43.1 0.0 copy-start.3
  43.1 0.6 %copy.24 = f32[8,512]{1,0:T(8,128)} copy(f32[8,512]{1,0:T(8,128)S(1)} %copy-done.4) | data formatting | bytes 32768
  43.7 0.1 copy-done.3
  43.9 0.6 %copy.25 = f32[8,512]{1,0:T(8,128)} copy(f32[8,512]{1,0:T(8,128)S(1)} %copy-done.3) | data formatting | bytes 32768
Async XLA Ops:
  38.1 2.4 %copy-start = (bf16[128,4096]{1,0:T(8,128)(2,1)S(1)}, bf16[128,4096]{1,0:T(8,128)(2,1)}, u32[]{:S(2)}) copy-start(bf16[128,4096]{1,0:T(8,128)(2,1)} %get-tuple-element.13) | copy-start | bytes 3145732
  40.4 1.0 %copy-start.2 = (bf16[128,512]{1,0:T(8,128)(2,1)S(1)}, bf16[128,512]{1,0:T(8,128)(2,1)}, u32[]{:S(2)}) copy-start(bf16[128,512]{1,0:T(8,128)(2,1)} %get-tuple-element.14) | copy-start | bytes 393220
  41.5 1.0 %copy-start.1 = (bf16[128,512]{1,0:T(8,128)(2,1)S(1)}, bf16[128,512]{1,0:T(8,128)(2,1)}, u32[]{:S(2)}) copy-start(bf16[128,512]{1,0:T(8,128)(2,1)} %get-tuple-element.15) | copy-start | bytes 393220
  42.4 0.7 %copy-start.4 = (f32[8,512]{1,0:T(8,128)S(1)}, f32[8,512]{1,0:T(8,128)}, u32[]{:S(2)}) copy-start(f32[8,512]{1,0:T(8,128)} %get-tuple-element.16) | copy-start | bytes 49156
  43.1 0.7 %copy-start.3 = (f32[8,512]{1,0:T(8,128)S(1)}, f32[8,512]{1,0:T(8,128)}, u32[]{:S(2)}) copy-start(f32[8,512]{1,0:T(8,128)} %get-tuple-element.17) | copy-start | bytes 49156

commit v2 on v1

--- a/solution.py
+++ b/solution.py
@@ -26,10 +26,11 @@
     n, kv_heads, group,
     q_hbm, og_hbm, ak, av, pk, pv, w, lens,
     attn_hbm, dq_hbm, akg, avg, pkg, pvg,
-    qv, ogv, attn_v, dq_v, win, pst, pgath, psend, precv, gsend, grecv, own,
+    qv, ogv, attn_v, dq_v, win, pst, pgath, psend, pmid, pred, precv,
+    gsend, gmid, gout, grecv, own,
     qs, cots, kcat, vcat, kt, vt, p_all, ds_all, bias, tri_b, wfull,
-    in_sem, out_sem, st_sem, win_send, win_recv, pg_send, pg_recv,
-    pr_send, pr_recv, gr_send, gr_recv,
+    in_sem, out_sem, st_sem, win_send, win_recv, wr_send, pg_send, pg_recv, pp_send, pp_recv,
+    pm_send, pm_recv, pr_send, pr_recv, gm_send, gm_recv, gr_send, gr_recv,
 ):
     me = lax.axis_index("row")
     height = ak.shape[0]
@@ -39,8 +40,20 @@
     factor = d ** (-0.5)
     log_factor = factor * math.log2(math.e)
 
-    def peer(k):
-        return lax.rem(me + k, n)
+    chips = n // 2
+    core = lax.rem(me, 2)
+    chip = me // 2
+    sibling = me + 1 - 2 * core
+    across = lax.rem(me + n - 1 + 2 * core, n)
+
+    def same(k):
+        return lax.rem(me + 2 * k, n)
+
+    def remote(src, dst, send, recv, target):
+        return pltpu.make_async_remote_copy(
+            src_ref=src, dst_ref=dst, send_sem=send, recv_sem=recv,
+            device_id={"row": target}, device_id_type=MESH,
+        )
 
     def cols(g, width):
         return pl.ds(pl.multiple_of(g * width, width), width)
@@ -64,50 +77,87 @@
         )
 
     def win_copy(g, far, which):
-        return pltpu.make_async_remote_copy(
-            src_ref=(ak, av)[which].at[:, cols(g, d)],
-            dst_ref=win.at[g, far, which],
-            send_sem=win_send.at[g, far, which],
-            recv_sem=win_recv.at[g, far, which],
-            device_id={"row": peer(1 + far)},
-            device_id_type=MESH,
+        return remote(
+            (ak, av)[which].at[:, cols(g, d)], win.at[g, far, which],
+            win_send.at[g, far, which], win_recv.at[g, far, which],
+            same(1) if far else lax.rem(me + 1, n),
+        )
+
+    def win_relay(g, which):
+        return remote(
+            win.at[g, 0, which], win.at[g, 1, which],
+            wr_send.at[g, which], win_recv.at[g, 1, which], sibling,
         )
 
     def gather_copy(g, k):
-        return pltpu.make_async_remote_copy(
-            src_ref=pst.at[g],
-            dst_ref=pgath.at[g, me],
-            send_sem=pg_send.at[g],
-            recv_sem=pg_recv.at[g],
-            device_id={"row": peer(k)},
-            device_id_type=MESH,
-        )
+        return remote(
+            pst.at[g], pgath.at[g, core, chip], pg_send.at[g], pg_recv.at[g], same(k)
+        )
+
+    def gather_relay(g):
+        return remote(
+            pgath.at[g, core], pgath.at[g, core], pp_send.at[g], pp_recv.at[g], sibling
+        )
+
+    def pair_copy(g):
+        return remote(psend.at[g, 1 - core], pmid.at[g], pm_send.at[g], pm_recv.at[g], sibling)
 
     def reduce_copy(g, k):
-        return pltpu.make_async_remote_copy(
-            src_ref=psend.at[g, peer(k)],
-            dst_ref=precv.at[g, me],
-            send_sem=pr_send.at[g],
-            recv_sem=pr_recv.at[g],
-            device_id={"row": peer(k)},
-            device_id_type=MESH,
-        )
+        return remote(
+            pred.at[g, lax.rem(chip + k, chips)], precv.at[g, chip],
+            pr_send.at[g], pr_recv.at[g], same(k),
+        )
+
+    def mid_copy(g):
+        return remote(gsend.at[g], gmid.at[g], gm_send.at[g], gm_recv.at[g], sibling)
 
     def back_copy(g, far):
-        return pltpu.make_async_remote_copy(
-            src_ref=gsend.at[g, far],
-            dst_ref=grecv.at[g, far],
-            send_sem=gr_send.at[g, far],
-            recv_sem=gr_recv.at[g, far],
-            device_id={"row": peer(n - 1 - far)},
-            device_id_type=MESH,
-        )
+        return remote(
+            gsend.at[g, 1] if far else gout.at[g], grecv.at[g],
+            gr_send.at[g, far], gr_recv.at[g], same(chips - 1) if far else across,
+        )
+
+    def relay(g):
+        for which in range(2):
+            win_copy(g, 0, which).wait_recv()
+
+        @pl.when(core == 0)
+        def _():
+            for which in range(2):
+                win_relay(g, which).start()
+
+        here = pgath.at[g, core]
+        pltpu.make_async_copy(here, here, pg_recv.at[g]).wait()
+        gather_relay(g).start()
+
+    def pass_on(g):
+        pair_copy(g).wait_recv()
+        pred[g] = (psend[g, core] + pmid[g]).astype(jnp.bfloat16)
+
+        @pl.when(core == 0)
+        def _():
+            mid_copy(g).wait_recv()
+            gout[g] = (
+                gsend[g, 0].astype(jnp.float32) + gmid[g, 1].astype(jnp.float32)
+            ).astype(jnp.bfloat16)
+            own[g] = own[g] + gmid[g, 0].astype(jnp.float32)
+            back_copy(g, 0).start()
+            back_copy(g, 1).start()
+
+        pltpu.make_async_copy(pred.at[g, chip], precv.at[g, chip], pr_recv.at[g]).start()
+
+        @pl.loop(1, chips)
+        def _(k):
+            reduce_copy(g, k).start()
 
     barrier = pltpu.get_barrier_semaphore()
 
-    @pl.loop(1, n)
+    @pl.loop(1, chips)
     def _(k):
-        pl.semaphore_signal(barrier, inc=1, device_id={"row": peer(k)}, device_id_type=MESH)
+        pl.semaphore_signal(barrier, inc=1, device_id={"row": same(k)}, device_id_type=MESH)
+
+    for target in (sibling, across):
+        pl.semaphore_signal(barrier, inc=1, device_id={"row": target}, device_id_type=MESH)
 
     for g in range(kv_heads):
         for copy in stage_copies(g):
@@ -140,22 +190,30 @@
     for g in range(kv_heads):
         for copy in stage_copies(g):
             copy.wait()
-    pl.semaphore_wait(barrier, n - 1)
+    pl.semaphore_wait(barrier, chips + 1)
 
     @pl.loop(0, kv_heads)
     def _(g):
-        pltpu.make_async_copy(pst.at[g], pgath.at[g, me], pg_recv.at[g]).start()
-
-        @pl.loop(1, n)
+        pltpu.make_async_copy(pst.at[g], pgath.at[g, core, chip], pg_recv.at[g]).start()
+
+        @pl.loop(1, chips)
         def _(k):
             gather_copy(g, k).start()
 
-        for far in range(2):
+        for which in range(2):
+            win_copy(g, 0, which).start()
+
+        @pl.when(core == 0)
+        def _():
             for which in range(2):
-                win_copy(g, far, which).start()
+                win_copy(g, 1, which).start()
 
     @pl.loop(0, kv_heads)
     def _(g):
+        @pl.when(g == 0)
+        def _():
+            relay(0)
+
         for copy in in_copies(g):
             copy.wait()
         for h in range(group):
@@ -163,13 +221,13 @@
             rows = slice(h * height, (h + 1) * height)
             qs[rows, :] = qv[g, :, lanes]
             cots[rows, :] = (wfull[...] * ogv[g, :, lanes].astype(jnp.float32)).astype(jnp.bfloat16)
-        pltpu.make_async_copy(pgath.at[g], pgath.at[g], pg_recv.at[g]).wait()
-        for far in range(2):
-            for which in range(2):
-                win_copy(g, far, which).wait_recv()
+        there = pgath.at[g, 1 - core]
+        pltpu.make_async_copy(there, there, pp_recv.at[g]).wait()
+        for which in range(2):
+            win_copy(g, 1, which).wait_recv()
         at1, at2, at3 = prompt, prompt + height, prompt + 2 * height
         for which, (cat, tr, mine) in enumerate(((kcat, kt, ak), (vcat, vt, av))):
-            gathered = pgath[g, :, which].astype(jnp.float32).reshape(prompt, d)
+            gathered = pgath[g, :, :, which].astype(jnp.float32).reshape(prompt, d)
             cat[:at1, :] = gathered.astype(jnp.bfloat16)
             cat[at1:at2, :] = win[g, 0, which]
             cat[at2:at3, :] = win[g, 1, which]
@@ -177,6 +235,15 @@
             tr[...] = cat[...].T
         tri2 = twice(tri)
         for pair in range(group // 2):
+            if pair == group // 4:
+                @pl.when(g > 0)
+                def _():
+                    pass_on(g - 1)
+
+                @pl.when(g < kv_heads - 1)
+                def _():
+                    relay(g + 1)
+
             rows = slice(pair * 2 * height, (pair + 1) * 2 * height)
             s = lax.dot_general(kcat[...], qs[rows, :], NT, preferred_element_type=jnp.float32)
             s_p = s[:at1]
@@ -229,28 +296,24 @@
                 part = dot(ds_all[...], qs[...]) * factor
             else:
                 part = dot(p_all[...], cots[...])
-            psend[g, :, which] = part[:at1].reshape(n, prompt // n, d).astype(jnp.bfloat16)
+            psend[g, :, :, which] = part[:at1].reshape(2, chips, prompt // n, d)
             gsend[g, 0, which] = part[at1:at2].astype(jnp.bfloat16)
             gsend[g, 1, which] = part[at2:at3].astype(jnp.bfloat16)
             own[g, which] = part[at3:]
-        back_copy(g, 1).start()
-        back_copy(g, 0).start()
-        pltpu.make_async_copy(psend.at[g, me], precv.at[g, me], pr_recv.at[g]).start()
-
-        @pl.loop(1, n)
-        def _(k):
-            reduce_copy(g, k).start()
-
+        pair_copy(g).start()
+
+        @pl.when(core == 1)
+        def _():
+            mid_copy(g).start()
+
+    pass_on(kv_heads - 1)
     for g in range(kv_heads):
         lanes = slice(g * d, (g + 1) * d)
-        for far in range(2):
-            back_copy(g, far).wait_recv()
+        back_copy(g, 0).wait_recv()
         for which, grad in enumerate((akg, avg)):
-            grad[:, lanes] = (
-                own[g, which]
-                + grecv[g, 0, which].astype(jnp.float32)
-                + grecv[g, 1, which].astype(jnp.float32)
-            ).astype(jnp.bfloat16)
+            grad[:, lanes] = (own[g, which] + grecv[g, which].astype(jnp.float32)).astype(
+                jnp.bfloat16
+            )
         pltpu.make_async_copy(precv.at[g], precv.at[g], pr_recv.at[g]).wait()
         for which, grad in enumerate((pkg, pvg)):
             grad[:, lanes] = jnp.sum(precv[g, :, which].astype(jnp.float32), axis=0)
@@ -258,14 +321,25 @@
     for g in range(kv_heads):
         for copy in out_copies(g):
             copy.wait()
-        for far in range(2):
-            back_copy(g, far).wait_send()
+        pair_copy(g).wait_send()
+        gather_relay(g).wait_send()
+        for which in range(2):
+            win_copy(g, 0, which).wait_send()
+        sent = pgath.at[g, 0, pl.ds(0, chips - 1)]
+        pltpu.make_async_copy(sent, sent, pg_send.at[g]).wait()
+        sent = precv.at[g, pl.ds(0, chips - 1)]
+        pltpu.make_async_copy(sent, sent, pr_send.at[g]).wait()
+
+        @pl.when(core == 0)
+        def _():
             for which in range(2):
-                win_copy(g, far, which).wait_send()
-        sent = pgath.at[g, pl.ds(0, n - 1)]
-        pltpu.make_async_copy(sent, sent, pg_send.at[g]).wait()
-        sent = precv.at[g, pl.ds(0, n - 1)]
-        pltpu.make_async_copy(sent, sent, pr_send.at[g]).wait()
+                win_copy(g, 1, which).wait_send()
+                win_relay(g, which).wait_send()
+                back_copy(g, which).wait_send()
+
+        @pl.when(core == 1)
+        def _():
+            mid_copy(g).wait_send()
 
 
 def per_device(n, queries, answer_keys, answer_values, prompt_keys, prompt_values, out_grad, weights, lengths):
@@ -300,11 +374,15 @@
             pltpu.VMEM((kv_heads, height, span), bf16),
             pltpu.VMEM((kv_heads, 2, 2, height, d), bf16),
             pltpu.VMEM((kv_heads, 2, own_prompt, d), bf16),
-            pltpu.VMEM((kv_heads, n, 2, own_prompt, d), bf16),
-            pltpu.VMEM((kv_heads, n, 2, own_prompt, d), bf16),
-            pltpu.VMEM((kv_heads, n, 2, own_prompt, d), bf16),
+            pltpu.VMEM((kv_heads, 2, n // 2, 2, own_prompt, d), bf16),
+            pltpu.VMEM((kv_heads, 2, n // 2, 2, own_prompt, d), f32),
+            pltpu.VMEM((kv_heads, n // 2, 2, own_prompt, d), f32),
+            pltpu.VMEM((kv_heads, n // 2, 2, own_prompt, d), bf16),
+            pltpu.VMEM((kv_heads, n // 2, 2, own_prompt, d), bf16),
             pltpu.VMEM((kv_heads, 2, 2, height, d), bf16),
             pltpu.VMEM((kv_heads, 2, 2, height, d), bf16),
+            pltpu.VMEM((kv_heads, 2, height, d), bf16),
+            pltpu.VMEM((kv_heads, 2, height, d), bf16),
             pltpu.VMEM((kv_heads, 2, height, d), f32),
             pltpu.VMEM((group * height, d), bf16),
             pltpu.VMEM((group * height, d), bf16),
@@ -322,12 +400,10 @@
             dma((kv_heads, 2)),
             dma((kv_heads, 2, 2)),
             dma((kv_heads, 2, 2)),
+            dma((kv_heads, 2)),
+            *[dma((kv_heads,))] * 10,
+            dma((kv_heads, 2)),
             dma((kv_heads,)),
-            dma((kv_heads,)),
-            dma((kv_heads,)),
-            dma((kv_heads,)),
-            dma((kv_heads, 2)),
-            dma((kv_heads, 2)),
         ],
         compiler_params=pltpu.CompilerParams(
             collective_id=0, has_side_effects=True, vmem_limit_bytes=60 * 1024 * 1024

time: 44.8 us -> 45 us (level)
  no operation moved by 1% of the time
where the time goes in v2:
time: 45 us; the launch traced here: 44.7 us
  Pallas kernels  37.7 us (84%)
  local copies, waits for them, and re-layouts  6.4 us (14%)
  between operations  0.66 us (1%)
    pallas_call x1, Pallas kernels, per_device(): pl.pallas_call(functools.partial(kernel, n, kv_heads, group), out_shape=(...  37.7 us
    unnamed x16, local copies, waits for them, and re-layouts  6.4 us

profile of v2, /device:TPU:0, one launch (start us, length us, event | category | flops | bytes accessed | tf_op | source)
XLA Modules:
  0.0 44.7 jit_solution(16469609251035249247)
XLA Ops:
  0.6 37.7 %shard_map.127 = (bf16[128,4096]{1,0:T(8,128)(2,1)}, bf16[128,4096]{1,0:T(8,128)(2,1)}, bf16[128,512]{1,0:T(8,128)(2,1)}, bf16[128,512]{1,0:T(8,128)(2,1)}, f32[8,512]{1,0:T(8,128)}, /*index=5*/f32[8,512]{1,0:T(8,128)}) custom-call(bf16[128,4096]{1,0:T(8,128)(2,1)} %q_hbm.1, bf16[128,4096]{1,0:T(8,128)(2,1)} %og_hbm.1, bf16[128,512]{1,0:T(8,128)(2,1)} %ak.1, ...), custom_call_target="tpu_custom_call" | custom-call | tf_op jit(solution)/shard_map/pallas_call | solution.py:358
  38.3 0.0 copy-start
  38.3 2.4 %copy.20 = bf16[128,4096]{1,0:T(8,128)(2,1)} copy(bf16[128,4096]{1,0:T(8,128)(2,1)} %get-tuple-element.12) | data formatting | bytes 2097152
  40.7 0.0 copy-done
  40.7 0.0 copy-start.2
  40.7 1.0 %copy.21 = bf16[128,4096]{1,0:T(8,128)(2,1)} copy(bf16[128,4096]{1,0:T(8,128)(2,1)S(1)} %copy-done) | data formatting | bytes 2097152
  41.7 0.1 copy-done.2
  41.7 0.0 copy-start.1
  41.7 0.7 %copy.22 = bf16[128,512]{1,0:T(8,128)(2,1)} copy(bf16[128,512]{1,0:T(8,128)(2,1)S(1)} %copy-done.2) | data formatting | bytes 262144
  42.4 0.3 copy-done.1
  42.7 0.0 copy-start.4
  42.7 0.7 %copy.23 = bf16[128,512]{1,0:T(8,128)(2,1)} copy(bf16[128,512]{1,0:T(8,128)(2,1)S(1)} %copy-done.1) | data formatting | bytes 262144
  43.3 0.1 copy-done.4
  43.4 0.0 copy-start.3
  43.4 0.6 %copy.24 = f32[8,512]{1,0:T(8,128)} copy(f32[8,512]{1,0:T(8,128)S(1)} %copy-done.4) | data formatting | bytes 32768
  44.0 0.1 copy-done.3
  44.1 0.6 %copy.25 = f32[8,512]{1,0:T(8,128)} copy(f32[8,512]{1,0:T(8,128)S(1)} %copy-done.3) | data formatting | bytes 32768
Async XLA Ops:
  38.3 2.4 %copy-start = (bf16[128,4096]{1,0:T(8,128)(2,1)S(1)}, bf16[128,4096]{1,0:T(8,128)(2,1)}, u32[]{:S(2)}) copy-start(bf16[128,4096]{1,0:T(8,128)(2,1)} %get-tuple-element.13) | copy-start | bytes 3145732
  40.7 1.0 %copy-start.2 = (bf16[128,512]{1,0:T(8,128)(2,1)S(1)}, bf16[128,512]{1,0:T(8,128)(2,1)}, u32[]{:S(2)}) copy-start(bf16[128,512]{1,0:T(8,128)(2,1)} %get-tuple-element.14) | copy-start | bytes 393220
  41.7 1.0 %copy-start.1 = (bf16[128,512]{1,0:T(8,128)(2,1)S(1)}, bf16[128,512]{1,0:T(8,128)(2,1)}, u32[]{:S(2)}) copy-start(bf16[128,512]{1,0:T(8,128)(2,1)} %get-tuple-element.15) | copy-start | bytes 393220
  42.7 0.7 %copy-start.4 = (f32[8,512]{1,0:T(8,128)S(1)}, f32[8,512]{1,0:T(8,128)}, u32[]{:S(2)}) copy-start(f32[8,512]{1,0:T(8,128)} %get-tuple-element.16) | copy-start | bytes 49156
  43.4 0.7 %copy-start.3 = (f32[8,512]{1,0:T(8,128)S(1)}, f32[8,512]{1,0:T(8,128)}, u32[]{:S(2)}) copy-start(f32[8,512]{1,0:T(8,128)} %get-tuple-element.17) | copy-start | bytes 49156

commit v3 on v2

--- a/solution.py
+++ b/solution.py
@@ -25,11 +25,11 @@
 def kernel(
     n, kv_heads, group,
     q_hbm, og_hbm, ak, av, pk, pv, w, lens,
-    attn_hbm, dq_hbm, akg, avg, pkg, pvg,
-    qv, ogv, attn_v, dq_v, win, pst, pgath, psend, pmid, pred, precv,
+    attn_v, dq_v, akg, avg, pkg, pvg,
+    qv, ogv, win, pst, pgath, psend, pmid, pred, precv,
     gsend, gmid, gout, grecv, own,
     qs, cots, kcat, vcat, kt, vt, p_all, ds_all, bias, tri_b, wfull,
-    in_sem, out_sem, st_sem, win_send, win_recv, wr_send, pg_send, pg_recv, pp_send, pp_recv,
+    in_sem, st_sem, win_send, win_recv, wr_send, pg_send, pg_recv, pp_send, pp_recv,
     pm_send, pm_recv, pr_send, pr_recv, gm_send, gm_recv, gr_send, gr_recv,
 ):
     me = lax.axis_index("row")
@@ -62,12 +62,6 @@
         return (
             pltpu.make_async_copy(q_hbm.at[:, cols(g, span)], qv.at[g], in_sem.at[g, 0]),
             pltpu.make_async_copy(og_hbm.at[:, cols(g, span)], ogv.at[g], in_sem.at[g, 1]),
-        )
-
-    def out_copies(g):
-        return (
-            pltpu.make_async_copy(attn_v.at[g], attn_hbm.at[:, cols(g, span)], out_sem.at[g, 0]),
-            pltpu.make_async_copy(dq_v.at[g], dq_hbm.at[:, cols(g, span)], out_sem.at[g, 1]),
         )
 
     def stage_copies(g):
@@ -289,8 +283,6 @@
                 lanes = slice((2 * pair + j) * d, (2 * pair + j + 1) * d)
                 attn_v[g, :, lanes] = out[j * height : (j + 1) * height]
                 dq_v[g, :, lanes] = dq[j * height : (j + 1) * height]
-        for copy in out_copies(g):
-            copy.start()
         for which in range(2):
             if which == 0:
                 part = dot(ds_all[...], qs[...]) * factor
@@ -319,8 +311,6 @@
             grad[:, lanes] = jnp.sum(precv[g, :, which].astype(jnp.float32), axis=0)
 
     for g in range(kv_heads):
-        for copy in out_copies(g):
-            copy.wait()
         pair_copy(g).wait_send()
         gather_relay(g).wait_send()
         for which in range(2):
@@ -340,6 +330,22 @@
         @pl.when(core == 1)
         def _():
             mid_copy(g).wait_send()
+
+
+def write_out(kv_heads, span, attn_v, dq_v, akg, avg, pkg, pvg, *refs):
+    outs, (wide_sem, sem) = refs[:6], refs[6:]
+    copies = [
+        pltpu.make_async_copy(v.at[g], out.at[:, pl.ds(g * span, span)], wide_sem.at[i, g])
+        for i, (v, out) in enumerate(((attn_v, outs[0]), (dq_v, outs[1])))
+        for g in range(kv_heads)
+    ] + [
+        pltpu.make_async_copy(v, out, sem.at[i])
+        for i, (v, out) in enumerate(zip((akg, avg, pkg, pvg), outs[2:]))
+    ]
+    for copy in copies:
+        copy.start()
+    for copy in copies:
+        copy.wait()
 
 
 def per_device(n, queries, answer_keys, answer_values, prompt_keys, prompt_values, out_grad, weights, lengths):
@@ -353,23 +359,21 @@
     span = group * d
     bf16, f32 = jnp.bfloat16, jnp.float32
     vmem = pl.BlockSpec(memory_space=pltpu.VMEM)
-    hbm = pl.BlockSpec(memory_space=pl.ANY)
+    hbm = pl.BlockSpec(memory_space=pltpu.HBM)
     dma = pltpu.SemaphoreType.DMA
-    return pl.pallas_call(
+    results = pl.pallas_call(
         functools.partial(kernel, n, kv_heads, group),
         out_shape=(
-            jax.ShapeDtypeStruct(queries.shape, bf16),
-            jax.ShapeDtypeStruct(queries.shape, bf16),
-            jax.ShapeDtypeStruct(answer_keys.shape, bf16),
-            jax.ShapeDtypeStruct(answer_keys.shape, bf16),
-            jax.ShapeDtypeStruct(prompt_keys.shape, f32),
-            jax.ShapeDtypeStruct(prompt_keys.shape, f32),
+            pltpu.VMEM((kv_heads, height, span), bf16),
+            pltpu.VMEM((kv_heads, height, span), bf16),
+            pltpu.VMEM(answer_keys.shape, bf16),
+            pltpu.VMEM(answer_keys.shape, bf16),
+            pltpu.VMEM(prompt_keys.shape, f32),
+            pltpu.VMEM(prompt_keys.shape, f32),
         ),
         in_specs=[hbm, hbm] + [vmem] * 6,
-        out_specs=(hbm, hbm) + (vmem,) * 4,
+        out_specs=(vmem,) * 6,
         scratch_shapes=[
-            pltpu.VMEM((kv_heads, height, span), bf16),
-            pltpu.VMEM((kv_heads, height, span), bf16),
             pltpu.VMEM((kv_heads, height, span), bf16),
             pltpu.VMEM((kv_heads, height, span), bf16),
             pltpu.VMEM((kv_heads, 2, 2, height, d), bf16),
@@ -397,7 +401,6 @@
             pltpu.VMEM((height, height), f32),
             dma((kv_heads, 2)),
             dma((kv_heads, 2)),
-            dma((kv_heads, 2)),
             dma((kv_heads, 2, 2)),
             dma((kv_heads, 2, 2)),
             dma((kv_heads, 2)),
@@ -412,6 +415,21 @@
         queries, out_grad, answer_keys, answer_values, prompt_keys, prompt_values,
         weights.reshape(1, height), lengths.reshape(1, lengths.shape[0]),
     )
+    return pl.pallas_call(
+        functools.partial(write_out, kv_heads, span),
+        out_shape=(
+            jax.ShapeDtypeStruct(queries.shape, bf16),
+            jax.ShapeDtypeStruct(queries.shape, bf16),
+            jax.ShapeDtypeStruct(answer_keys.shape, bf16),
+            jax.ShapeDtypeStruct(answer_keys.shape, bf16),
+            jax.ShapeDtypeStruct(prompt_keys.shape, f32),
+            jax.ShapeDtypeStruct(prompt_keys.shape, f32),
+        ),
+        in_specs=[vmem] * 6,
+        out_specs=(hbm,) * 6,
+        scratch_shapes=[dma((2, kv_heads)), dma((4,))],
+        compiler_params=pltpu.CompilerParams(vmem_limit_bytes=4 * 1024 * 1024),
+    )(*results)
 
 
 def solution(mesh):

time: 45 us -> 39.2 us (0.87)
  local copies, waits for them, and re-layouts: 6.4 us -> 0 us
  Pallas kernels: 37.7 us -> 38.4 us
    unnamed x16 -> x0, local copies, waits for them, and re-layouts: 6.4 us -> none
    pallas_call x0 -> x1, Pallas kernels: none -> 1.51 us  [per_device(): pl.pallas_call(functools.partial(write_out, kv_heads, span), out_shape=(j...]
    pallas_call x1, Pallas kernels: 37.7 us -> 36.9 us  [per_device(): pl.pallas_call(functools.partial(kernel, n, kv_heads, group), out_shape=(...]
where the time goes in v3:
time: 39.2 us; the launch traced here: 39.1 us
  Pallas kernels  38.4 us (98%)
  between operations  0.64 us (2%)
    pallas_call x1, Pallas kernels, per_device(): pl.pallas_call(functools.partial(kernel, n, kv_heads, group), out_shape=(...  36.9 us
    pallas_call x1, Pallas kernels, per_device(): pl.pallas_call(functools.partial(write_out, kv_heads, span), out_shape=(j...  1.51 us

profile of v3, /device:TPU:0, one launch (start us, length us, event | category | flops | bytes accessed | tf_op | source)
XLA Modules:
  0.0 39.1 jit_solution(5529748019921876336)
XLA Ops:
  0.6 36.9 %shard_map.127 = (bf16[4,128,1024]{2,1,0:T(8,128)(2,1)S(1)}, bf16[4,128,1024]{2,1,0:T(8,128)(2,1)S(1)}, bf16[128,512]{1,0:T(8,128)(2,1)S(1)}, bf16[128,512]{1,0:...) custom-call(bf16[128,4096]{1,0:T(8,128)(2,1)} %q_hbm.1, bf16[128,4096]{1,0:T(8,128)(2,1)} %og_hbm.1, ...), custom_call_target="tpu_custom_call" | custom-call | tf_op jit(solution)/shard_map/pallas_call | solution.py:364
  37.5 1.5 %shard_map.128 = (bf16[128,4096]{1,0:T(8,128)(2,1)}, bf16[128,4096]{1,0:T(8,128)(2,1)}, bf16[128,512]{1,0:T(8,128)(2,1)}, bf16[128,512]{1,0:T(8,128)(2,1)}, f32[8,512]{1,0:T(8,128)}, /*index=5*/f32[8,512]{1,0:T(8,128)}) custom-call(bf16[4,128,1024]{2,1,0:T(8,128)(2,1)S(1)} %get-tuple-element.12.attn_v, bf16[4,128,1024]{2,1,0:T(8,128)(2,1)S(1)} %get-tuple-element.13.dq_v, ...), custom_call_target="tpu_custom_call" | custom-call | tf_op jit(solution)/shard_map/pallas_call | solution.py:418

commit v4 on v3

--- a/solution.py
+++ b/solution.py
@@ -26,9 +26,9 @@
     n, kv_heads, group,
     q_hbm, og_hbm, ak, av, pk, pv, w, lens,
     attn_v, dq_v, akg, avg, pkg, pvg,
-    qv, ogv, win, pst, pgath, psend, pmid, pred, precv,
+    ogv, win, pst, pgath, psend, pmid, pred, precv,
     gsend, gmid, gout, grecv, own,
-    qs, cots, kcat, vcat, kt, vt, p_all, ds_all, bias, tri_b, wfull,
+    qs, cots, cots_t, kcat, vcat, kt, vt, p_all, ds_all, bias, tri_b, wfull,
     in_sem, st_sem, win_send, win_recv, wr_send, pg_send, pg_recv, pp_send, pp_recv,
     pm_send, pm_recv, pr_send, pr_recv, gm_send, gm_recv, gr_send, gr_recv,
 ):
@@ -58,11 +58,14 @@
     def cols(g, width):
         return pl.ds(pl.multiple_of(g * width, width), width)
 
-    def in_copies(g):
-        return (
-            pltpu.make_async_copy(q_hbm.at[:, cols(g, span)], qv.at[g], in_sem.at[g, 0]),
-            pltpu.make_async_copy(og_hbm.at[:, cols(g, span)], ogv.at[g], in_sem.at[g, 1]),
-        )
+    def q_copy(g, h):
+        return pltpu.make_async_copy(
+            q_hbm.at[:, pl.ds((g * group + h) * d, d)],
+            qs.at[g, pl.ds(h * height, height)], in_sem.at[g, 0],
+        )
+
+    def og_copy(g):
+        return pltpu.make_async_copy(og_hbm.at[:, cols(g, span)], ogv.at[g], in_sem.at[g, 1])
 
     def stage_copies(g):
         return (
@@ -157,8 +160,10 @@
         for copy in stage_copies(g):
             copy.start()
     for g in range(kv_heads):
-        for copy in in_copies(g):
-            copy.start()
+        og_copy(g).start()
+    for g in range(kv_heads):
+        for h in range(group):
+            q_copy(g, h).start()
 
     answers = lens.shape[1]
     row = lax.broadcasted_iota(jnp.int32, (answers, answers), 0)
@@ -181,6 +186,19 @@
     tri_b[...] = tri.astype(jnp.float32).astype(jnp.bfloat16)
     wfull[...] = jnp.broadcast_to(w[...], (height, height)).T
 
+    def prepare(g):
+        og_copy(g).wait()
+        for h in range(group):
+            rows = slice(h * height, (h + 1) * height)
+            cot = wfull[...] * ogv[g, :, h * d : (h + 1) * d].astype(jnp.float32)
+            cot = cot.astype(jnp.bfloat16)
+            cots[g, rows, :] = cot
+            cots_t[g, :, rows] = cot.T
+
+    @pl.loop(0, kv_heads)
+    def _(g):
+        prepare(g)
+
     for g in range(kv_heads):
         for copy in stage_copies(g):
             copy.wait()
@@ -202,19 +220,12 @@
             for which in range(2):
                 win_copy(g, 1, which).start()
 
+    relay(0)
+
     @pl.loop(0, kv_heads)
     def _(g):
-        @pl.when(g == 0)
-        def _():
-            relay(0)
-
-        for copy in in_copies(g):
-            copy.wait()
-        for h in range(group):
-            lanes = slice(h * d, (h + 1) * d)
-            rows = slice(h * height, (h + 1) * height)
-            qs[rows, :] = qv[g, :, lanes]
-            cots[rows, :] = (wfull[...] * ogv[g, :, lanes].astype(jnp.float32)).astype(jnp.bfloat16)
+        mine = qs.at[g]
+        pltpu.make_async_copy(mine, mine, in_sem.at[g, 0]).wait()
         there = pgath.at[g, 1 - core]
         pltpu.make_async_copy(there, there, pp_recv.at[g]).wait()
         for which in range(2):
@@ -229,17 +240,8 @@
             tr[...] = cat[...].T
         tri2 = twice(tri)
         for pair in range(group // 2):
-            if pair == group // 4:
-                @pl.when(g > 0)
-                def _():
-                    pass_on(g - 1)
-
-                @pl.when(g < kv_heads - 1)
-                def _():
-                    relay(g + 1)
-
             rows = slice(pair * 2 * height, (pair + 1) * 2 * height)
-            s = lax.dot_general(kcat[...], qs[rows, :], NT, preferred_element_type=jnp.float32)
+            s = lax.dot_general(kcat[...], qs[g, rows, :], NT, preferred_element_type=jnp.float32)
             s_p = s[:at1]
             s_1 = s[at1:at2] + twice(bias[0])
             s_c = jnp.where(tri2, s[at3:], s[at2:at3]) + twice(bias[1])
@@ -265,7 +267,7 @@
             p_all[at2:at3, rows] = b_c - b_d
             p_all[at3:, rows] = b_d
             out_t = dot(vt[...], p_all[:, rows]).astype(jnp.bfloat16)
-            cot_t = cots[rows, :].T
+            cot_t = cots_t[g, :, rows]
             delta = jnp.sum(
                 cot_t.astype(jnp.float32) * out_t.astype(jnp.float32), axis=0, keepdims=True
             )
@@ -277,17 +279,15 @@
             g_d = g_c * trib2
             ds_all[at2:at3, rows] = g_c - g_d
             ds_all[at3:, rows] = g_d
-            dq_t = (dot(kt[...], ds_all[:, rows]) * factor).astype(jnp.bfloat16)
-            out, dq = out_t.T, dq_t.T
+            out = out_t.T
             for j in range(2):
                 lanes = slice((2 * pair + j) * d, (2 * pair + j + 1) * d)
                 attn_v[g, :, lanes] = out[j * height : (j + 1) * height]
-                dq_v[g, :, lanes] = dq[j * height : (j + 1) * height]
         for which in range(2):
             if which == 0:
-                part = dot(ds_all[...], qs[...]) * factor
+                part = dot(ds_all[...], qs[g]) * factor
             else:
-                part = dot(p_all[...], cots[...])
+                part = dot(p_all[...], cots[g])
             psend[g, :, :, which] = part[:at1].reshape(2, chips, prompt // n, d)
             gsend[g, 0, which] = part[at1:at2].astype(jnp.bfloat16)
             gsend[g, 1, which] = part[at2:at3].astype(jnp.bfloat16)
@@ -298,7 +298,16 @@
         def _():
             mid_copy(g).start()
 
-    pass_on(kv_heads - 1)
+        @pl.when(g < kv_heads - 1)
+        def _():
+            relay(g + 1)
+
+        dq_t = (dot(kt[...], ds_all[...]) * factor).astype(jnp.bfloat16)
+        for h in range(group):
+            rows = slice(h * height, (h + 1) * height)
+            dq_v[g, :, h * d : (h + 1) * d] = dq_t[:, rows].T
+        pass_on(g)
+
     for g in range(kv_heads):
         lanes = slice(g * d, (g + 1) * d)
         back_copy(g, 0).wait_recv()
@@ -375,7 +384,6 @@
         out_specs=(vmem,) * 6,
         scratch_shapes=[
             pltpu.VMEM((kv_heads, height, span), bf16),
-            pltpu.VMEM((kv_heads, height, span), bf16),
             pltpu.VMEM((kv_heads, 2, 2, height, d), bf16),
             pltpu.VMEM((kv_heads, 2, own_prompt, d), bf16),
             pltpu.VMEM((kv_heads, 2, n // 2, 2, own_prompt, d), bf16),
@@ -388,8 +396,9 @@
             pltpu.VMEM((kv_heads, 2, height, d), bf16),
             pltpu.VMEM((kv_heads, 2, height, d), bf16),
             pltpu.VMEM((kv_heads, 2, height, d), f32),
-            pltpu.VMEM((group * height, d), bf16),
-            pltpu.VMEM((group * height, d), bf16),
+            pltpu.VMEM((kv_heads, group * height, d), bf16),
+            pltpu.VMEM((kv_heads, group * height, d), bf16),
+            pltpu.VMEM((kv_heads, d, group * height), bf16),
             pltpu.VMEM((keys, d), bf16),
             pltpu.VMEM((keys, d), bf16),
             pltpu.VMEM((d, keys), bf16),

time: 39.2 us -> 34.3 us (0.87)
  Pallas kernels: 38.4 us -> 33.5 us
    pallas_call x1, Pallas kernels: 36.9 us -> 32 us  [per_device(): pl.pallas_call(functools.partial(kernel, n, kv_heads, group), out_shape=(...]
where the time goes in v4:
time: 34.3 us; the launch traced here: 34.1 us
  Pallas kernels  33.5 us (98%)
  between operations  0.64 us (2%)
    pallas_call x1, Pallas kernels, per_device(): pl.pallas_call(functools.partial(kernel, n, kv_heads, group), out_shape=(...  32 us
    pallas_call x1, Pallas kernels, per_device(): pl.pallas_call(functools.partial(write_out, kv_heads, span), out_shape=(j...  1.51 us

profile of v4, /device:TPU:0, one launch (start us, length us, event | category | flops | bytes accessed | tf_op | source)
XLA Modules:
  0.0 34.1 jit_solution(12443456806373229625)
XLA Ops:
  0.6 32.0 %shard_map.127 = (bf16[4,128,1024]{2,1,0:T(8,128)(2,1)S(1)}, bf16[4,128,1024]{2,1,0:T(8,128)(2,1)S(1)}, bf16[128,512]{1,0:T(8,128)(2,1)S(1)}, bf16[128,512]{1,0:...) custom-call(bf16[128,4096]{1,0:T(8,128)(2,1)} %q_hbm.1, bf16[128,4096]{1,0:T(8,128)(2,1)} %og_hbm.1, ...), custom_call_target="tpu_custom_call" | custom-call | tf_op jit(solution)/shard_map/pallas_call | solution.py:373
  32.6 1.5 %shard_map.128 = (bf16[128,4096]{1,0:T(8,128)(2,1)}, bf16[128,4096]{1,0:T(8,128)(2,1)}, bf16[128,512]{1,0:T(8,128)(2,1)}, bf16[128,512]{1,0:T(8,128)(2,1)}, f32[8,512]{1,0:T(8,128)}, /*index=5*/f32[8,512]{1,0:T(8,128)}) custom-call(bf16[4,128,1024]{2,1,0:T(8,128)(2,1)S(1)} %get-tuple-element.12.attn_v, bf16[4,128,1024]{2,1,0:T(8,128)(2,1)S(1)} %get-tuple-element.13.dq_v, ...), custom_call_target="tpu_custom_call" | custom-call | tf_op jit(solution)/shard_map/pallas_call | solution.py:427
